TPU v7x, 128 devices: a whole 4x4x4 slice. The times are simulated.
128 devices in a mesh: lat: 4 (over y), lon: 16 (over z, x), mem: 2 (over core).
Axes of the slice: x: 4, y: 4, z: 4, core: 2. Of those that a mesh axis runs over, the one named last changes fastest.
Arguments:
- anomalies: bfloat16 [24, 16, 1440, 512], P('mem', None, 'lon', 'lat'), may hold values from -6 to 6
- taper: float32 [16, 1440, 512], P('lon', 'lat'), may hold values from 0.5 to 8
- obs_row: int32 [256, 2048], P('lat', 'lon'), may hold values from 0 to 511, as said below
- obs_col: int32 [256, 2048], P('lat', 'lon'), may hold values from 0 to 1439, as said below
- obs_level: int32 [256, 2048], P('lat', 'lon'), may hold values from 0 to 15
- obs_value: float32 [256, 2048], P('lat', 'lon'), may hold values from -18 to 18
Outputs:
- increment: float32 [16, 1440, 512], P(None, 'lon', 'lat')
Inputs may be any that keep to these rules, and one draw needn't show every extreme that they name: `obs_row`: the entry in row i lies in latitude rows (i // 64) * 128 to (i // 64 + 1) * 128 - 1, drawn evenly there. `obs_col`: the entry in column j lies in longitude columns (j // 128) * 90 to (j // 128 + 1) * 90 - 1, drawn evenly there.
All inputs are finite; a program needn't handle non-finite values.
Results may differ from a plain program's by a relative error of at most 0.0066.
Values may be sent and summed in bfloat16 or wider, within the bound.
No kernel may reach another device: no remote copies, remote signals or barrier semaphores. Data moves between devices by JAX's collectives and lax.ppermute only.
A program may use at most 128 MiB of HBM per device.

v0:
```python
import math

import jax
import jax.numpy as jnp
from jax import lax
from jax.experimental import pallas as pl
from jax.experimental.pallas import tpu as pltpu
from jax.sharding import PartitionSpec as P


BF = jnp.bfloat16
F32 = jnp.float32
LL = ("lat", "lon")
SWAP = [(0, 1), (1, 0)]
RING = 4


def vspec():
    return pl.BlockSpec(memory_space=pltpu.VMEM)


def sspec():
    return pl.BlockSpec(memory_space=pltpu.SMEM)


def params(mib, **more):
    return pltpu.CompilerParams(vmem_limit_bytes=mib * 1024 * 1024, **more)


def cost(flops):
    return pl.CostEstimate(flops=int(flops), bytes_accessed=1 << 20, transcendentals=0)


def over_all(x):
    return lax.all_to_all(x, LL, split_axis=0, concat_axis=0, tiled=True)


def shift_lat(x, s):
    return lax.ppermute(x, "lat", [(i, (i + s) % RING) for i in range(RING)])


def beside_pairs():
    turns = (1, RING - 1)
    return [(2 * i + m, 2 * ((i + turns[m]) % RING) + m) for i in range(RING) for m in range(2)]


def swap(x):
    return lax.ppermute(x, "mem", SWAP)


LEAD = 6


def turn_block(blocks, turn, levels):
    both = jnp.concatenate([block.reshape(16 * levels, 128) for block in blocks], axis=1)
    return jnp.dot(turn, both, preferred_element_type=F32).astype(BF)


def turner(levels, mirrored, have):
    size = 16 * levels
    to = lax.broadcasted_iota(jnp.int32, (size, size), 0)
    frm = lax.broadcasted_iota(jnp.int32, (size, size), 1)
    within = to & 15
    taken = jnp.where(mirrored, 15 - within, within)
    return jnp.where((frm == taken * levels + (to >> 4)) & (within < have), 1.0, 0.0).astype(BF)


def turn_start(start, mirrored, cols):
    return jnp.where(mirrored, LEAD + cols - 15 - start, LEAD + start)


def head_kernel(fields, row_hbm, col_hbm, level_hbm, value_hbm, out, *scratch, half, levels, cols, padded):
    row_ref, col_ref, level_ref, value_ref, fields_in, staged, innov, acc, sems = scratch
    bands = fields.shape[1]
    count = iter(range(32))

    def fetch(source, target):
        copy = pltpu.make_async_copy(source, target, sems.at[next(count)])
        copy.start()
        return copy

    observed = [
        fetch(row_hbm, row_ref),
        fetch(col_hbm, col_ref),
        fetch(level_hbm, level_ref),
        fetch(value_hbm, value_ref),
    ]
    arriving = [
        (
            fetch(fields.at[pl.ds(0, 2), g], fields_in.at[:, g, pl.ds(LEAD, cols)]),
            fetch(fields.at[pl.ds(0, 2), g, pl.ds(0, 1)], fields_in.at[:, g, pl.ds(LEAD + cols, 1)]),
        )
        for g in range(bands)
    ]
    mem, lat, lon = lax.axis_index("mem"), lax.axis_index("lat"), lax.axis_index("lon")
    mirrored = lon >= lax.axis_size("lon") // 2
    for p in range(2):
        for g in range(bands):
            fields_in[p, g, :LEAD] = jnp.zeros((LEAD, levels, 128), BF)
            fields_in[p, g, LEAD + cols + 1 :] = jnp.zeros((LEAD - 1, levels, 128), BF)
    slots = levels * half
    acc[...] = jnp.zeros_like(acc)

    def spots_of(count):
        major = lax.broadcasted_iota(jnp.int32, (count // 16, 16, 128), 0)
        minor = lax.broadcasted_iota(jnp.int32, (count // 16, 16, 128), 1)
        return (major * 16 + minor).astype(F32).astype(BF)

    def packed(row):
        return jnp.broadcast_to(row, (16, 128)).astype(BF)[None]

    slot_ids = spots_of(256)
    row_ids = spots_of(128)
    one = jnp.ones((), BF)
    zero = jnp.zeros((), BF)
    for copy in observed:
        copy.wait()

    def add_group(g, carry):
        rows = pl.ds(pl.multiple_of(g * 16, 8), 16)
        column = col_ref[rows, :] - lon * cols
        within = jnp.where(mirrored & (column > 0), cols - column, column) - mem * half
        inside = (within >= 0) & (within < half)
        keys = jnp.where(inside, level_ref[rows, :] * half + within, -1)
        lat_row = (row_ref[rows, :] - lat * 128).astype(F32)
        value = value_ref[rows, :]
        high = value.astype(BF).astype(F32)
        middle = value - high
        parts = []
        for start in range(0, slots, 256):
            part = keys - start
            parts.append(jnp.where((part >= 0) & (part < 256), part, -1).astype(F32))
        left = []
        right = []
        for r in range(16):
            at = slice(r, r + 1)
            hits = [jnp.where(slot_ids == packed(part[at]), one, zero).reshape(256, 128) for part in parts]
            left.append(jnp.concatenate(hits, axis=0))
            row_hit = row_ids == packed(lat_row[at])
            sides = [jnp.where(row_hit, packed(side[at]), zero).reshape(128, 128) for side in (high, middle)]
            right.append(jnp.concatenate(sides, axis=0))
        acc[...] += lax.dot_general(
            jnp.concatenate(left, axis=1),
            jnp.concatenate(right, axis=1),
            (((1,), (1,)), ((), ())),
            preferred_element_type=F32,
        )
        return carry

    leaving = []
    lax.fori_loop(0, 2, add_group, 0)
    turn = turner(levels, mirrored, 16)
    last_turn = turner(levels, mirrored, cols % 16)
    for first in range(0, bands, 2):
        group = range(first, first + 2)
        for g in group:
            for copy in arriving[g]:
                copy.wait()
        for start in range(0, padded, 16):
            rows = pl.ds(turn_start(start, mirrored, cols), 16)
            matrix = turn if start + 16 <= cols else last_turn
            turned = turn_block([fields_in[p, g, rows] for g in group for p in range(2)], matrix, levels)
            for l in range(levels):
                for n, g in enumerate(group):
                    for p in range(2):
                        lane = 256 * n + 128 * p
                        piece = turned[16 * l : 16 * l + 16, lane : lane + 128]
                        staged[g * levels + l, p * padded + start : p * padded + start + 16, :] = piece
        for g in group:
            leaving.append(
                fetch(
                    staged.at[pl.ds(g * levels, levels)],
                    out.at[pl.ds(g * levels, levels), pl.ds(0, 2 * padded), :],
                )
            )
    lax.fori_loop(2, row_ref.shape[0] // 16, add_group, 0)
    innov[...] = (acc[:, :128] + acc[:, 128:]).astype(BF).reshape(levels, half, 128)
    leaving += [
        fetch(innov, out.at[pl.ds(g * levels, levels), pl.ds(2 * padded, half), :]) for g in range(bands)
    ]
    for copy in leaving:
        copy.wait()


def head(fields, obs_row, obs_col, obs_level, obs_value, half, padded):
    _, bands, cols, levels, lanes = fields.shape
    rows = 2 * padded + half
    hbm = pl.BlockSpec(memory_space=pltpu.HBM)
    observed = (obs_row, obs_col, obs_level, obs_value)
    return pl.pallas_call(
        lambda *refs: head_kernel(*refs, half=half, levels=levels, cols=cols, padded=padded),
        out_shape=jax.ShapeDtypeStruct((bands * levels, rows, lanes), BF),
        in_specs=[hbm] * 5,
        out_specs=hbm,
        scratch_shapes=[pltpu.VMEM(array.shape, array.dtype) for array in observed]
        + [
            pltpu.VMEM((2, bands, cols + 2 * LEAD, levels, lanes), BF),
            pltpu.VMEM((bands * levels, 2 * padded, lanes), BF),
            pltpu.VMEM((levels, half, lanes), BF),
            pltpu.VMEM((levels * half, 2 * lanes), F32),
            pltpu.SemaphoreType.DMA((32,)),
        ],
        compiler_params=params(61),
        cost_estimate=cost(6e9),
        name="head",
    )(fields, *observed)


def relayout_last_kernel(place, in_ref, out_ref, room, *, cols, levels, padded):
    mirrored = place[2] >= place[3]
    for p in range(2):
        room[p, :LEAD] = jnp.zeros((LEAD, levels, 128), BF)
        room[p, LEAD : LEAD + cols] = in_ref[0, p]
        room[p, LEAD + cols] = in_ref[0, p, 0]
        room[p, LEAD + cols + 1 :] = jnp.zeros((LEAD - 1, levels, 128), BF)
    turn = turner(levels, mirrored, 16)
    last_turn = turner(levels, mirrored, cols % 16)
    for start in range(0, padded, 16):
        rows = pl.ds(turn_start(start, mirrored, cols), 16)
        matrix = turn if start + 16 <= cols else last_turn
        turned = turn_block([room[p, rows] for p in range(2)], matrix, levels)
        for l in range(levels):
            for p in range(2):
                piece = turned[16 * l : 16 * l + 16, 128 * p : 128 * p + 128]
                out_ref[p * levels + l, start : start + 16, :] = piece


def relayout_last(place, fields, padded):
    rounds, bands, cols, levels, lanes = fields.shape
    return pl.pallas_call(
        lambda *refs: relayout_last_kernel(*refs, cols=cols, levels=levels, padded=padded),
        grid=(bands // 2,),
        in_specs=[sspec(), pl.BlockSpec((1, 2, cols, levels, lanes), lambda g: (rounds - 1, g, 0, 0, 0))],
        out_specs=pl.BlockSpec((2 * levels, padded, lanes), lambda g: (g, 0, 0)),
        out_shape=jax.ShapeDtypeStruct((bands * levels, padded, lanes), BF),
        scratch_shapes=[pltpu.VMEM((2, cols + 2 * LEAD, levels, lanes), BF)],
        compiler_params=params(58),
        name="relayout_last",
    )(place, fields)


def turn_cos(turns):
    near = 0.25 - jnp.abs(turns - jnp.floor(turns + 0.5))
    square = near * near
    value = jnp.full_like(square, -15.094642576822990)
    for factor in (42.058693944897653, -76.705859753061386, 81.605249276075055, -41.341702240399755):
        value = value * square + factor
    return near * (value * square + 6.283185307179586)


def basis_kernel(lon_ref, lon_t_ref, lat_ref, lat_t_ref, *, cols, blocks, padded):
    total = cols * blocks
    nyquist = total // 2
    width = lon_ref.shape[1] // 2
    lanes = lax.broadcasted_iota(jnp.int32, (padded, 128), 1)

    def turns_of(product):
        whole = (product.astype(F32) * (1.0 / total)).astype(jnp.int32)
        return (product - whole * total).astype(F32) * (1.0 / total)

    def lon_rows(j, carry):
        within = lax.broadcasted_iota(jnp.int32, (padded, 128), 0)
        x = jnp.where(within < cols, within + cols * j, cols * (blocks - 1 - j))
        fine = turns_of(x * lanes)
        coarse = turns_of(x * (lanes * 128))
        fine_cos = turn_cos(fine)
        fine_sin = turn_cos(fine - 0.25)
        scale = jnp.where(within <= cols, math.sqrt(2.0 / total), 0.0)
        coarse_cos = turn_cos(coarse) * scale
        coarse_sin = turn_cos(coarse - 0.25) * scale
        rows = pl.ds(pl.multiple_of(j * padded, padded), padded)
        for t in range(width // 128):
            c = lanes + 128 * t
            cos_t = coarse_cos[:, t : t + 1]
            sin_t = coarse_sin[:, t : t + 1]
            even = fine_cos * cos_t - fine_sin * sin_t
            odd = fine_sin * cos_t + fine_cos * sin_t
            if t == 0 or 128 * t <= nyquist < 128 * t + 128:
                even = jnp.where((c == 0) | (c == nyquist), even * math.sqrt(0.5), even)
            if 128 * t + 127 >= nyquist:
                even = jnp.where(c <= nyquist, even, 0.0)
                odd = jnp.where(c < nyquist, odd, 0.0)
            lon_ref[rows, 128 * t : 128 * t + 128] = even.astype(BF)
            lon_ref[rows, width + 128 * t : width + 128 * t + 128] = odd.astype(BF)
        return carry

    lax.fori_loop(0, blocks // 2, lon_rows, 0)
    for t in range(lon_ref.shape[1] // 128):
        strip = lon_ref[:, 128 * t : 128 * t + 128].astype(F32)
        lon_t_ref[128 * t : 128 * t + 128, :] = strip.T.astype(BF)

    length = lat_ref.shape[0]
    step = 64

    def lat_rows(i, carry):
        shape = (step, length)
        down = lax.broadcasted_iota(jnp.int32, shape, 0) + step * i
        across = lax.broadcasted_iota(jnp.int32, shape, 1)
        rows = pl.ds(pl.multiple_of(i * step, step), step)
        for grid, mode, ref in ((down, across, lat_ref), (across, down, lat_t_ref)):
            phase = (mode * (2 * grid + 1)) & (4 * length - 1)
            scale = jnp.where(mode == 0, 1.0 / math.sqrt(length), math.sqrt(2.0 / length))
            ref[rows, :] = (turn_cos(phase.astype(F32) * (0.25 / length)) * scale).astype(BF)
        return carry

    lax.fori_loop(0, length // step, lat_rows, 0)


def bases(cols, blocks, padded, lat_total):
    tall = padded * blocks // 2
    return pl.pallas_call(
        lambda *refs: basis_kernel(*refs, cols=cols, blocks=blocks, padded=padded),
        out_shape=(
            jax.ShapeDtypeStruct((tall, 2 * tall), BF),
            jax.ShapeDtypeStruct((2 * tall, tall), BF),
            jax.ShapeDtypeStruct((lat_total, lat_total), BF),
            jax.ShapeDtypeStruct((lat_total, lat_total), BF),
        ),
        out_specs=(vspec(),) * 4,
        compiler_params=params(58),
        cost_estimate=cost(12e9),
        name="bases",
    )()


def arrange_kernel(place, band, own, other, taper, *, rows_each):
    mem, lat = place[0], place[1]
    spare = taper.shape[1] - RING * rows_each
    taper[:, RING * rows_each :, :] = jnp.zeros((4, spare, 128), BF)

    def rows_of(turn):
        return pl.ds(pl.multiple_of(lax.rem(lat + turn, RING) * rows_each, 8), rows_each)

    for q in range(4):
        taper[q, rows_of(0), :] = band[:, 128 * q : 128 * q + 128]
    for ref, side in ((own, mem), (other, 1 - mem)):
        beside = rows_of(jnp.where(side == 0, RING - 1, 1))
        for q in range(4):
            taper[q, beside, :] = ref[q // 2, :, 128 * (q % 2) : 128 * (q % 2) + 128]
        for q in range(2):
            taper[2 * side + q, rows_of(2), :] = ref[2, :, 128 * q : 128 * q + 128]


def arrange(place, band, own, other):
    rows_each = own.shape[1]
    return pl.pallas_call(
        lambda *refs: arrange_kernel(*refs, rows_each=rows_each),
        out_shape=jax.ShapeDtypeStruct((4, RING * rows_each + 32, 128), BF),
        in_specs=[sspec(), vspec(), vspec(), vspec()],
        out_specs=vspec(),
        compiler_params=params(12),
        cost_estimate=cost(1e9),
        name="arrange",
    )(place, band, own, other)


def member_kernel(*refs, first, final, count, blocks, bands, padded, coefs):
    place, field_in, own_in, other_in, taper_hbm, lon_hbm, lon_t_hbm, lat_hbm, lat_t_hbm = refs[:9]
    rest = list(refs[9:])
    so_far_hbm = None if first else rest.pop(0)
    outs = [rest.pop(0) for _ in range(2 if final else 1)]
    folded, inverse, taper, lon_ref, lon_t_ref, lat_ref, lat_t_ref, acc, sems = rest[:9]
    stages = rest[9:10]
    field, own, other = (field_in, own_in, other_in) if final else rest[10:]
    pairs = blocks // 2
    tall = padded * pairs
    nyquist = coefs // 2
    parts = 4
    step = (nyquist // 2 + 16) // 16 * 16
    group = 4
    turns = pairs // group
    half = padded // 2
    mem = place[0]

    def move(source, target, spot):
        return pltpu.make_async_copy(source, target, sems.at[spot])

    def lon_t_copy(r):
        rows = pl.ds(pl.multiple_of((r // 2) * tall + (r % 2) * step, 16), step)
        return move(lon_t_hbm.at[rows], lon_t_ref.at[rows], 10 + r)

    def lon_copy(b):
        rows = pl.ds(pl.multiple_of(b * group * padded, padded), group * padded)
        return move(lon_hbm.at[rows], lon_ref.at[rows], 14 + b)

    def spots(b, side):
        return pl.ds((blocks - group - b * group) if side else b * group, group)

    def so_far_copy(b, side):
        at = spots(b, side)
        return move(so_far_hbm.at[:, at], acc.at[:, at], 18 + 2 * b + side)

    def out_copy(b, side, n):
        at = spots(b, side)
        stage = stages[0].at[n] if final else stages[0]
        return move(stage.at[:, at], outs[n].at[:, at], 22 + 4 * n + 2 * b + side)

    field_copies = []
    if not final:
        field_copies = [
            move(own_in, own, 0),
            move(other_in, other, 1),
            *[move(field_in.at[a, :, pl.ds(0, count * padded), :], field.at[a], 2 + a) for a in range(bands)],
        ]
    table_copies = [
        lon_t_copy(0),
        lon_t_copy(2),
        move(lat_hbm, lat_ref, 7),
        move(taper_hbm, taper, 8),
        move(lat_t_hbm, lat_t_ref, 9),
    ]
    for copy in field_copies + table_copies:
        copy.start()
    for side in range(2):
        inverse[side, 2 * step :, :] = jnp.zeros((tall - 2 * step, inverse.shape[2]), BF)
    for copy in field_copies:
        copy.wait()
    down = lax.broadcasted_iota(jnp.int32, (padded, 128), 0)
    cols = coefs // blocks

    def weigh(i, a):
        def product(j):
            mine, theirs = own[a, j], other[a, j]
            innov = jnp.concatenate(
                [jnp.where(mem == 0, mine, theirs), jnp.where(mem == 0, theirs, mine)], axis=0
            )
            return field[a, j, i * padded : (i + 1) * padded, :].astype(F32) * innov.astype(F32)

        def body(j, carry):
            rows = pl.ds(pl.multiple_of(j * padded, padded), padded)
            near = product(j)
            far = product(blocks - 1 - j)
            near = jnp.where(down == cols, far[0:1, :], near)
            far = jnp.where(down == 0, 0.0, far)
            folded[0, rows, 128 * a : 128 * a + 128] = (near + far).astype(BF)
            folded[1, rows, 128 * a : 128 * a + 128] = (near - far).astype(BF)
            return carry

        lax.fori_loop(0, pairs, body, 0)

    def spectral(fresh):
        def body(r, carry):
            rows = pl.ds(pl.multiple_of(r * step, 16), step)
            if fresh:

                @pl.when(r > 0)
                def _():
                    for side in range(2):
                        lon_t_copy(2 * side + r).wait()

            tables = [pl.ds(pl.multiple_of(side * tall + r * step, 16), step) for side in range(2)]
            zonal = [
                jnp.dot(lon_t_ref[tables[side], :], folded[side], preferred_element_type=F32).astype(BF)
                for side in range(2)
            ]
            if fresh:

                @pl.when(r == 0)
                def _():
                    for copy in table_copies[2:]:
                        copy.wait()

            spectrum = [jnp.dot(zonal[side], lat_ref[...], preferred_element_type=F32) for side in range(2)]
            tapered = []
            for side in range(2):
                weight_rows = pl.ds(pl.multiple_of(side * nyquist + r * step, 16), step)
                weights = jnp.concatenate([taper[q, weight_rows, :] for q in range(4)], axis=1).astype(F32)
                tapered.append((spectrum[side] * weights).astype(BF))
            for side in range(2):
                back = jnp.dot(tapered[side], lat_t_ref[...], preferred_element_type=F32)
                inverse[side, rows, :] = back.astype(BF)
            if fresh:

                @pl.when(r == 0)
                def _():
                    for b in range(turns):
                        lon_copy(b).start()
                        if not first:
                            so_far_copy(b, 0).start()
                            so_far_copy(b, 1).start()

            return carry

        lax.fori_loop(0, parts // 2, body, 0)

    def gridded(i):
        def body(b, carry):
            rows = pl.ds(pl.multiple_of(b * group * padded, padded), group * padded)
            if i == 0:
                lon_copy(b).wait()
                if not first:
                    so_far_copy(b, 0).wait()
                    so_far_copy(b, 1).wait()
            even = jnp.dot(lon_ref[rows, :tall], inverse[0], preferred_element_type=F32)
            odd = jnp.dot(lon_ref[rows, tall:], inverse[1], preferred_element_type=F32)

            def put(piece, a, j):
                piece = piece * field[a, j, i * padded : (i + 1) * padded, :].astype(F32)
                piece = piece if first and i == 0 else piece + acc[a, j].astype(F32)
                if final:
                    stages[0][mem, a, j] = piece[:half].astype(BF)
                    stages[0][1 - mem, a, j] = piece[half:].astype(BF)
                elif i == count - 1:
                    stages[0][a, j] = piece.astype(BF)
                else:
                    acc[a, j] = piece

            for g in range(group):
                for a in range(bands):
                    j = b * group + g
                    spot = (slice(g * padded, (g + 1) * padded), slice(128 * a, 128 * a + 128))
                    near = even[spot] + odd[spot]
                    far = jnp.where(down == 0, near[cols : cols + 1, :], even[spot] - odd[spot])
                    put(near, a, j)
                    put(far, a, blocks - 1 - j)
            if i == count - 1:
                for n in range(len(outs)):
                    out_copy(b, 0, n).start()
                    out_copy(b, 1, n).start()
            return carry

        for b in range(turns):
            body(b, 0)

    for i in range(count):
        if i == 0:
            for r in (1, 3):
                lon_t_copy(r).start()
        for a in range(bands):
            weigh(i, a)
        if i == 0:
            for copy in table_copies[:2]:
                copy.wait()
        spectral(i == 0)
        gridded(i)
    for b in range(turns):
        for n in range(len(outs)):
            out_copy(b, 0, n).wait()
            out_copy(b, 1, n).wait()


def member(place, field, own, other, taper, tables, so_far, final, dims):
    _, blocks, bands, padded, coefs, lat_total = dims
    half = padded // 2
    tall = padded * blocks // 2
    first = so_far is None
    count = 1 if final else 2
    split = lambda array: array.reshape(bands, blocks, *array.shape[1:])
    near = [split(field), split(own), split(other)]
    far = [taper, *tables] + ([] if first else [so_far])
    block = lambda rows, dtype: ((bands, blocks, rows, 128), dtype)
    scratch = [((2, tall, lat_total), BF), ((2, tall, lat_total), BF)]
    fields = [] if final else [block(count * padded, BF), block(half, BF), block(half, BF)]
    scratch += [(array.shape, array.dtype) for array in (taper, *tables)]
    scratch.append(block(padded, F32 if first else BF))
    results = [block(half, BF), block(half, BF)] if final else [block(padded, BF)]
    staged = ((2, bands, blocks, half, 128), BF) if final else block(padded, BF)
    hbm = pl.BlockSpec(memory_space=pltpu.HBM)
    return pl.pallas_call(
        lambda *refs: member_kernel(
            *refs, first=first, final=final, count=count, blocks=blocks, bands=bands, padded=padded, coefs=coefs
        ),
        out_shape=[jax.ShapeDtypeStruct(*each) for each in results],
        in_specs=[sspec()] + [vspec() if final else hbm] * len(near) + [hbm] * len(far),
        out_specs=[hbm] * len(results),
        scratch_shapes=[pltpu.VMEM(*each) for each in scratch]
        + [pltpu.SemaphoreType.DMA((32,))]
        + [pltpu.VMEM(*each) for each in [staged, *fields]],
        compiler_params=params(63),
        cost_estimate=cost(count * 6e9),
        name="member_last" if final else "member_pair",
    )(place, *near, *far)


def finish_kernel(place, own, other, out, *, levels, cols, half, scale):
    mem = place[0]
    mirrored = place[2] >= place[3]
    bands = own.shape[0] // levels
    to = lax.broadcasted_iota(jnp.int32, (2 * half, half), 0)
    frm = lax.broadcasted_iota(jnp.int32, (2 * half, half), 1)
    taken = jnp.where(mirrored & (to > 0), cols - to, to)
    picks = [jnp.where(taken == frm + side * half, 1.0, 0.0).astype(BF) for side in (mem, 1 - mem)]
    picks = jnp.concatenate(picks * bands, axis=1)
    columns = []
    for l in range(levels):
        parts = [ref[a * levels + l] for a in range(bands) for ref in (own, other)]
        columns.append(jnp.concatenate(parts, axis=0))
    summed = jnp.dot(picks, jnp.concatenate(columns, axis=1), preferred_element_type=F32) * scale
    for l in range(levels):
        out[:, l, :] = summed[:cols, 128 * l : 128 * l + 128]


def finish(place, own, other, levels, cols, half, scale):
    return pl.pallas_call(
        lambda *refs: finish_kernel(*refs, levels=levels, cols=cols, half=half, scale=scale),
        out_shape=jax.ShapeDtypeStruct((cols, levels, 128), F32),
        in_specs=[sspec(), vspec(), vspec()],
        out_specs=vspec(),
        compiler_params=params(16),
        name="finish",
    )(place, own, other)


def local(anomalies, taper, obs_row, obs_col, obs_level, obs_value):
    members, levels, cols, lat_rows = anomalies.shape
    bands = lax.axis_size("lat")
    blocks = lax.axis_size("lon")
    mem, lat, lon = lax.axis_index("mem"), lax.axis_index("lat"), lax.axis_index("lon")
    coefs = cols * blocks
    lat_total = lat_rows * bands
    padded = -(-cols // 32) * 32
    half = padded // 2
    ensemble = members * lax.axis_size("mem")
    place = jnp.stack([mem, lat, lon, jnp.int32(blocks // 2)]).astype(jnp.int32)

    by_round = jnp.transpose(anomalies, (0, 2, 1, 3)).reshape(members // bands, bands, cols, levels, lat_rows)
    pair_out = head(by_round, obs_row, obs_col, obs_level, obs_value, half, padded)
    pair_out, taper = lax.optimization_barrier((pair_out, taper))
    pair = over_all(pair_out)
    n_half = lat_total // 2
    band = taper[0].astype(BF)
    band_half = lax.dynamic_slice_in_dim(taper[0], mem * n_half, n_half, axis=1).astype(BF)
    beside = lax.ppermute(band, ("lat", "mem"), beside_pairs())
    across = shift_lat(band_half, 2)
    last_out = relayout_last(place, by_round, padded)
    last = over_all(last_out)
    held = jnp.stack([beside[:, :n_half], beside[:, n_half:], across])
    weights = arrange(place, band, held, swap(held))
    own = pair[:, 2 * padded :, :]
    other = swap(own)

    tables = bases(cols, blocks, padded, lat_total)
    dims = (cols, blocks, bands, padded, coefs, lat_total)
    (summed,) = member(place, pair, own, other, weights, tables, None, False, dims)
    mine, theirs = member(place, last, own, other, weights, tables, summed, True, dims)
    merged = (mine.astype(F32) + swap(theirs).astype(F32)).astype(BF).reshape(bands * blocks, half, lat_rows)
    pieces = over_all(merged)
    out = finish(place, pieces, swap(pieces), levels, cols, half, 1.0 / (ensemble - 1))
    return jnp.transpose(out, (1, 0, 2))


def solution(mesh):
    in_specs = (
        P("mem", None, "lon", "lat"),
        P("lon", "lat", None),
        P("lat", "lon"),
        P("lat", "lon"),
        P("lat", "lon"),
        P("lat", "lon"),
    )
    out_specs = P(None, "lon", "lat")

    return jax.shard_map(local, mesh=mesh, in_specs=in_specs, out_specs=out_specs, check_vma=False)
```

profile of v0, /device:TPU:1, one launch (start us, length us, event | category | flops | bytes accessed | tf_op | source)
XLA Modules:
  0.0 156.5 jit_solution(14091415961558199126)
XLA Ops:
  0.0 7.4 %head.1 = bf16[64,240,128]{2,1,0:T(8,128)(2,1)} custom-call(bf16[3,4,90,16,128]{4,3,2,1,0:T(8,128)(2,1)} %bitcast.21, s32[64,128]{1,0:T(8,128)} %refs_1_.1, s32[64,128]{1,0:T(8,128)} %refs_2_.1, s32[64,128]{1,0:T(8,128)} %refs_3_.1, f32[64,128]{1,0:T(8,128)} %refs_4_.1), custom_call_target="tpu_custom_call" | custom-call | flops 6000000000 | bytes 1048576 | tf_op jit(solution)/shard_map/head/pallas_call | solution.py:190
  7.4 0.0 copy-start.3
  7.4 12.3 %all-to-all-start.1 = ((bf16[64,240,128]{2,1,0:T(8,128)(2,1)}), bf16[64,240,128]{2,1,0:T(8,128)(2,1)}, u32[]{:S(2)}, u32[]{:S(2)}) async-start(bf16[64,240,128]{2,1,0:T(8,128)(2,1)} %head.1), calls=%async_computation.1 | async-start | bytes 7864320 | tf_op jit(solution)/shard_map/all_to_all | solution.py:35
  19.7 0.0 copy-done.3
  19.8 2.4 %collective-permute-start.1 = (bf16[360,512]{1,0:T(8,128)(2,1)S(1)}, bf16[360,512]{1,0:T(8,128)(2,1)S(1)}, u32[]{:S(2)}, u32[]{:S(2)}) collective-permute-start(bf16[360,512]{1,0:T(8,128)(2,1)S(1)} %convert_bitcast_fusion.refs_1_), channel_id=1, source_target_pairs={{0,32},{1,97},{32,64},{33,1},{64,96},{65,33},{96,0},{97,65},{2,34}... | collective-permute-start | bytes 1105928 | tf_op jit(solution)/shard_map/ppermute | solution.py:623
  22.2 0.5 collective-permute-start.2
  22.7 0.6 pad_add_fusion.refs_0_
  23.3 3.0 %relayout_last.1 = bf16[64,96,128]{2,1,0:T(8,128)(2,1)} custom-call(s32[4]{0:T(128)} %pad_add_fusion.refs_0_, bf16[3,4,90,16,128]{4,3,2,1,0:T(8,128)(2,1)} %bitcast.22), custom_call_target="tpu_custom_call" | custom-call | tf_op jit(solution)/shard_map/relayout_last/pallas_call | solution.py:230
  26.3 44.1 %collective-permute-done.1 = bf16[360,512]{1,0:T(8,128)(2,1)S(1)} collective-permute-done((bf16[360,512]{1,0:T(8,128)(2,1)S(1)}, bf16[360,512]{1,0:T(8,128)(2,1)S(1)}, u32[]{:S(2)}, u32[]{:S(2)}) %collective-permute-start.1) | collective-permute-done | bytes 368672 | tf_op jit(solution)/shard_map/ppermute | solution.py:623
  70.4 0.0 collective-permute-done.2
  70.4 0.1 pad_maximum_fusion.refs_2_
  70.5 4.2 %collective-permute-start.3 = (bf16[3,360,256]{2,1,0:T(8,128)(2,1)S(1)}, bf16[3,360,256]{2,1,0:T(8,128)(2,1)S(1)}, u32[]{:S(2)}, u32[]{:S(2)}) collective-permute-start(bf16[3,360,256]{2,1,0:T(8,128)(2,1)S(1)} %pad_maximum_fusion.refs_2_), channel_id=1, source_target_pairs={{0,1},{1,0},{2,3},{3,2},{4,5},{5,4},{6,7},{7,6},{8,9},{9,8},{10,11... | collective-permute-start | bytes 1658888 | tf_op jit(solution)/shard_map/ppermute | solution.py:48
  74.7 0.0 all-to-all-done.1
  74.7 9.8 %all-to-all-start = ((bf16[64,96,128]{2,1,0:T(8,128)(2,1)}), bf16[64,96,128]{2,1,0:T(8,128)(2,1)}, u32[]{:S(2)}, u32[]{:S(2)}) async-start(bf16[64,96,128]{2,1,0:T(8,128)(2,1)} %relayout_last.1), calls=%async_computation | async-start | bytes 3145728 | tf_op jit(solution)/shard_map/all_to_all | solution.py:35
  84.6 1.2 slice.12
  85.8 0.0 copy-start.4
  85.8 0.0 copy-start
  85.8 0.6 collective-permute-start
  86.4 7.0 %bases.1 = (bf16[768,1536]{1,0:T(8,128)(2,1)}, bf16[1536,768]{1,0:T(8,128)(2,1)}, bf16[512,512]{1,0:T(8,128)(2,1)}, bf16[512,512]{1,0:T(8,128)(2,1)}) custom-call(), custom_call_target="tpu_custom_call" | custom-call | flops 12000000000 | bytes 1048576 | tf_op jit(solution)/shard_map/bases/pallas_call | solution.py:311
  93.4 0.0 copy-done.4
  93.4 0.0 collective-permute-done.3.refs_3_
  93.4 0.0 copy-done
  93.4 0.8 arrange.1.refs_4_
  94.3 0.0 copy-start.2
  94.3 1.1 copy-done.2
  95.4 0.0 collective-permute-done
  95.4 0.0 copy-start.5
  95.4 0.9 copy-done.5
  96.3 15.6 %member_pair.1.refs_9_ = bf16[4,16,96,128]{3,2,1,0:T(8,128)(2,1)} custom-call(s32[4]{0:T(128)} %pad_add_fusion.refs_0_, bf16[4,16,240,128]{3,2,1,0:T(8,128)(2,1)} %bitcast.14.refs_1_, bf16[4,16,48,128]{3,2,1,0:T(8,128)(2,1)} %bitcast.24, bf16[4,16,48,128]{3,2,1,0:T(8,128)(2,1)} %bitcast.27, bf16[4,1472,128]{2,1,0:T(8,128)(2,1)} %copy-done.2, ...), custom_call_target="tpu_custom_call" | custom-call | flops 12000000000 | bytes 1048576 | tf_op jit(solution)/shard_map/member_pair/pallas_call | solution.py:559
  112.0 0.0 all-to-all-done
  112.0 9.6 %member_last.1 = (bf16[4,16,48,128]{3,2,1,0:T(8,128)(2,1)}, bf16[4,16,48,128]{3,2,1,0:T(8,128)(2,1)}) custom-call(s32[4]{0:T(128)} %pad_add_fusion.refs_0_, bf16[4,16,96,128]{3,2,1,0:T(8,128)(2,1)} %bitcast.5.refs_1_, bf16[4,16,48,128]{3,2,1,0:T(8,128)(2,1)} %bitcast.25, bf16[4,16,48,128]{3,2,1,0:T(8,128)(2,1)} %bitcast.28, bf16[4,1472,128]{2,1,0:T(8,128)(2,1)} %copy-done.2, ...), custom_call_target="tpu_custom_call" | custom-call | flops 6000000000 | bytes 1048576 | tf_op jit(solution)/shard_map/member_last/pallas_call | solution.py:559
  121.6 0.2 collective-permute-start.4
  121.8 2.4 %collective-permute-done.4 = bf16[4,16,48,128]{3,2,1,0:T(8,128)(2,1)S(1)} collective-permute-done((bf16[4,16,48,128]{3,2,1,0:T(8,128)(2,1)}, bf16[4,16,48,128]{3,2,1,0:T(8,128)(2,1)S(1)}, u32[]{:S(2)}, u32[]{:S(2)}) %collective-permute-start.4) | collective-permute-done | bytes 786464 | tf_op jit(solution)/shard_map/ppermute | solution.py:48
  124.2 0.0 copy-start.1
  124.2 1.3 add_convert_fusion
  125.5 25.4 %all_to_all.15.refs_1_ = bf16[64,48,128]{2,1,0:T(8,128)(2,1)S(1)} all-to-all(bf16[64,48,128]{2,1,0:T(8,128)(2,1)S(1)} %bitcast.23), channel_id=1, replica_groups=mesh['lat'=4,'lon'=16,'mem'=2] {'lat','lon'}, dimensions={0} | all-to-all | bytes 1572864 | tf_op jit(solution)/shard_map/all_to_all | solution.py:35
  150.9 1.6 %collective-permute-start.5 = (bf16[64,48,128]{2,1,0:T(8,128)(2,1)S(1)}, bf16[64,48,128]{2,1,0:T(8,128)(2,1)S(1)}, u32[]{:S(2)}, u32[]{:S(2)}) collective-permute-start(bf16[64,48,128]{2,1,0:T(8,128)(2,1)S(1)} %all_to_all.15.refs_1_), channel_id=1, source_target_pairs={{0,1},{1,0},{2,3},{3,2},{4,5},{5,4},{6,7},{7,6},{8,9},{9,8},{10,11... | collective-permute-start | bytes 2359304 | tf_op jit(solution)/shard_map/ppermute | solution.py:48
  152.5 1.9 %collective-permute-done.5.refs_2_ = bf16[64,48,128]{2,1,0:T(8,128)(2,1)S(1)} collective-permute-done((bf16[64,48,128]{2,1,0:T(8,128)(2,1)S(1)}, bf16[64,48,128]{2,1,0:T(8,128)(2,1)S(1)}, u32[]{:S(2)}, u32[]{:S(2)}) %collective-permute-start.5) | collective-permute-done | bytes 786464 | tf_op jit(solution)/shard_map/ppermute | solution.py:48
  154.4 0.0 copy-done.1
  154.4 2.1 %finish.1 = f32[90,16,128]{2,1,0:T(8,128)} custom-call(s32[4]{0:T(128)S(1)} %copy-done.1, bf16[64,48,128]{2,1,0:T(8,128)(2,1)S(1)} %all_to_all.15.refs_1_, bf16[64,48,128]{2,1,0:T(8,128)(2,1)S(1)} %collective-permute-done.5.refs_2_), custom_call_target="tpu_custom_call" | custom-call | tf_op jit(solution)/shard_map/finish/pallas_call | solution.py:594
  (3 shorter events, 0.1 us)
Async XLA Ops:
  7.4 12.4 %copy-start.3 = (f32[1,360,512]{2,1,0:T(8,128)S(1)}, f32[1,360,512]{2,1,0:T(8,128)}, u32[]{:S(2)}) copy-start(f32[1,360,512]{2,1,0:T(8,128)} %param.7) | copy-start | bytes 2211844
  7.4 67.3 %all-to-all-start.1 = ((bf16[64,240,128]{2,1,0:T(8,128)(2,1)}), bf16[64,240,128]{2,1,0:T(8,128)(2,1)}, u32[]{:S(2)}, u32[]{:S(2)}) async-start(bf16[64,240,128]{2,1,0:T(8,128)(2,1)} %head.1), calls=%async_computation.1 | async-start | bytes 7864320 | tf_op jit(solution)/shard_map/all_to_all | solution.py:35
  19.8 50.6 %collective-permute-start.1 = (bf16[360,512]{1,0:T(8,128)(2,1)S(1)}, bf16[360,512]{1,0:T(8,128)(2,1)S(1)}, u32[]{:S(2)}, u32[]{:S(2)}) collective-permute-start(bf16[360,512]{1,0:T(8,128)(2,1)S(1)} %convert_bitcast_fusion.refs_1_), channel_id=1, source_target_pairs={{0,32},{1,97},{32,64},{33,1},{64,96},{65,33},{96,0},{97,65},{2,34}... | collective-permute-start | bytes 1105928 | tf_op jit(solution)/shard_map/ppermute | solution.py:623
  22.2 48.2 %collective-permute-start.2 = (bf16[360,256]{1,0:T(8,128)(2,1)S(1)}, bf16[360,256]{1,0:T(8,128)(2,1)S(1)}, u32[]{:S(2)}, u32[]{:S(2)}) collective-permute-start(bf16[360,256]{1,0:T(8,128)(2,1)S(1)} %fusion), channel_id=1, source_target_pairs={{0,64},{32,96},{64,0},{96,32},{1,65},{33,97},{65,1},{97,33},{2,66}... | collective-permute-start | bytes 552968 | tf_op jit(solution)/shard_map/ppermute | solution.py:39
  70.5 22.9 %collective-permute-start.3 = (bf16[3,360,256]{2,1,0:T(8,128)(2,1)S(1)}, bf16[3,360,256]{2,1,0:T(8,128)(2,1)S(1)}, u32[]{:S(2)}, u32[]{:S(2)}) collective-permute-start(bf16[3,360,256]{2,1,0:T(8,128)(2,1)S(1)} %pad_maximum_fusion.refs_2_), channel_id=1, source_target_pairs={{0,1},{1,0},{2,3},{3,2},{4,5},{5,4},{6,7},{7,6},{8,9},{9,8},{10,11... | collective-permute-start | bytes 1658888 | tf_op jit(solution)/shard_map/ppermute | solution.py:48
  74.7 37.3 %all-to-all-start = ((bf16[64,96,128]{2,1,0:T(8,128)(2,1)}), bf16[64,96,128]{2,1,0:T(8,128)(2,1)}, u32[]{:S(2)}, u32[]{:S(2)}) async-start(bf16[64,96,128]{2,1,0:T(8,128)(2,1)} %relayout_last.1), calls=%async_computation | async-start | bytes 3145728 | tf_op jit(solution)/shard_map/all_to_all | solution.py:35
  85.8 7.7 %copy-start.4 = (bf16[64,48,128]{2,1,0:T(8,128)(2,1)}, bf16[64,48,128]{2,1,0:T(8,128)(2,1)S(1)}, u32[]{:S(2)}) copy-start(bf16[64,48,128]{2,1,0:T(8,128)(2,1)S(1)} %slice.12) | copy-start | bytes 2359300
  85.8 7.7 %copy-start = (s32[4]{0:T(128)S(1)}, s32[4]{0:T(128)}, u32[]{:S(2)}) copy-start(s32[4]{0:T(128)} %pad_add_fusion.refs_0_) | copy-start | bytes 52
  85.8 9.6 %collective-permute-start = (bf16[64,48,128]{2,1,0:T(8,128)(2,1)S(1)}, bf16[64,48,128]{2,1,0:T(8,128)(2,1)S(1)}, u32[]{:S(2)}, u32[]{:S(2)}) collective-permute-start(bf16[64,48,128]{2,1,0:T(8,128)(2,1)S(1)} %slice.12), channel_id=1, source_target_pairs={{0,1},{1,0},{2,3},{3,2},{4,5},{5,4},{6,7},{7,6},{8,9},{9,8},{10,11... | collective-permute-start | bytes 2359304 | tf_op jit(solution)/shard_map/ppermute | solution.py:48
  94.3 1.1 copy-start.2
  95.4 0.9 copy-start.5
  121.6 2.6 %collective-permute-start.4 = (bf16[4,16,48,128]{3,2,1,0:T(8,128)(2,1)}, bf16[4,16,48,128]{3,2,1,0:T(8,128)(2,1)S(1)}, u32[]{:S(2)}, u32[]{:S(2)}) collective-permute-start(bf16[4,16,48,128]{3,2,1,0:T(8,128)(2,1)} %get-tuple-element.20), channel_id=1, source_target_pairs={{0,1},{1,0},{2,3},{3,2},{4,5},{5,4},{6,7},{7,6},{8,9},{9,8},{10,11... | collective-permute-start | bytes 2359304 | tf_op jit(solution)/shard_map/ppermute | solution.py:48
  124.2 30.2 %copy-start.1 = (s32[4]{0:T(128)S(1)}, s32[4]{0:T(128)}, u32[]{:S(2)}) copy-start(s32[4]{0:T(128)} %pad_add_fusion.refs_0_) | copy-start | bytes 52
  150.9 3.5 %collective-permute-start.5 = (bf16[64,48,128]{2,1,0:T(8,128)(2,1)S(1)}, bf16[64,48,128]{2,1,0:T(8,128)(2,1)S(1)}, u32[]{:S(2)}, u32[]{:S(2)}) collective-permute-start(bf16[64,48,128]{2,1,0:T(8,128)(2,1)S(1)} %all_to_all.15.refs_1_), channel_id=1, source_target_pairs={{0,1},{1,0},{2,3},{3,2},{4,5},{5,4},{6,7},{7,6},{8,9},{9,8},{10,11... | collective-permute-start | bytes 2359304 | tf_op jit(solution)/shard_map/ppermute | solution.py:48
where the time goes:
time: 157 us
  waiting for transfers between devices  48.4 us (31%)
  Pallas kernels  45.6 us (29%)
  starting transfers between devices  31.7 us (20%)
  blocking collectives  25.4 us (16%)
  local copies, waits for them, and re-layouts  3.32 us (2%)
  other arithmetic  2.07 us (1%)
    ppermute x1, waiting for transfers between devices, local(): beside = lax.ppermute(band, ('lat', 'mem'), beside_pairs())  44.1 us
    all_to_all x1, blocking collectives, over_all(): return lax.all_to_all(x, LL, split_axis=0, concat_axis=0, tiled=True)  25.4 us
    pallas_call x2, Pallas kernels, member(): pl.pallas_call(lambda *refs: member_kernel(*refs, first=first, final=fina...  25.3 us
    all_to_all x2, starting transfers between devices, over_all(): return lax.all_to_all(x, LL, split_axis=0, concat_axis=0, tiled=True)  22.2 us
    pallas_call x1, Pallas kernels, head(): pl.pallas_call(lambda *refs: head_kernel(*refs, half=half, levels=levels,...  7.35 us
    pallas_call x1, Pallas kernels, bases(): pl.pallas_call(lambda *refs: basis_kernel(*refs, cols=cols, blocks=blocks...  7.02 us
    ppermute x4, starting transfers between devices, swap(): return lax.ppermute(x, 'mem', SWAP)  6.61 us
    ppermute x4, waiting for transfers between devices, swap(): return lax.ppermute(x, 'mem', SWAP)  4.28 us
  transfers between devices with their start and end apart: 8, of which 3 were waited for; matrix products, arithmetic and copies ran while one was open for 1% of the time, Pallas kernels for 17%

commit v1 on v0

--- a/solution.py
+++ b/solution.py
@@ -355,11 +355,11 @@
 
 
 def member_kernel(*refs, first, final, count, blocks, bands, padded, coefs):
-    place, field_in, own_in, other_in, taper_hbm, lon_hbm, lon_t_hbm, lat_hbm, lat_t_hbm = refs[:9]
+    place, field_in, own_in, other_in, taper_hbm, lon_hbm, lon_t_hbm, lat_hbm, _ = refs[:9]
     rest = list(refs[9:])
     so_far_hbm = None if first else rest.pop(0)
     outs = [rest.pop(0) for _ in range(2 if final else 1)]
-    folded, inverse, taper, lon_ref, lon_t_ref, lat_ref, lat_t_ref, acc, sems = rest[:9]
+    folded, inverse, taper, lon_ref, lon_t_ref, lat_ref, _, acc, sems = rest[:9]
     stages = rest[9:10]
     field, own, other = (field_in, own_in, other_in) if final else rest[10:]
     pairs = blocks // 2
@@ -407,7 +407,6 @@
         lon_t_copy(2),
         move(lat_hbm, lat_ref, 7),
         move(taper_hbm, taper, 8),
-        move(lat_t_hbm, lat_t_ref, 9),
     ]
     for copy in field_copies + table_copies:
         copy.start()
@@ -467,18 +466,10 @@
                 weights = jnp.concatenate([taper[q, weight_rows, :] for q in range(4)], axis=1).astype(F32)
                 tapered.append((spectrum[side] * weights).astype(BF))
             for side in range(2):
-                back = jnp.dot(tapered[side], lat_t_ref[...], preferred_element_type=F32)
+                back = lax.dot_general(
+                    tapered[side], lat_ref[...], (((1,), (1,)), ((), ())), preferred_element_type=F32
+                )
                 inverse[side, rows, :] = back.astype(BF)
-            if fresh:
-
-                @pl.when(r == 0)
-                def _():
-                    for b in range(turns):
-                        lon_copy(b).start()
-                        if not first:
-                            so_far_copy(b, 0).start()
-                            so_far_copy(b, 1).start()
-
             return carry
 
         lax.fori_loop(0, parts // 2, body, 0)
@@ -531,6 +522,11 @@
         if i == 0:
             for copy in table_copies[:2]:
                 copy.wait()
+            for b in range(turns):
+                lon_copy(b).start()
+                if not first:
+                    so_far_copy(b, 0).start()
+                    so_far_copy(b, 1).start()
         spectral(i == 0)
         gridded(i)
     for b in range(turns):

time: 157 us -> 157 us (level)
  no operation moved by 1% of the time
where the time goes in v1:
time: 157 us
  waiting for transfers between devices  48.4 us (31%)
  Pallas kernels  45.6 us (29%)
  starting transfers between devices  31.7 us (20%)
  blocking collectives  25.4 us (16%)
  local copies, waits for them, and re-layouts  3.32 us (2%)
  other arithmetic  2.07 us (1%)
    ppermute x1, waiting for transfers between devices, local(): beside = lax.ppermute(band, ('lat', 'mem'), beside_pairs())  44.1 us
    all_to_all x1, blocking collectives, over_all(): return lax.all_to_all(x, LL, split_axis=0, concat_axis=0, tiled=True)  25.4 us
    pallas_call x2, Pallas kernels, member(): pl.pallas_call(lambda *refs: member_kernel(*refs, first=first, final=fina...  25.3 us
    all_to_all x2, starting transfers between devices, over_all(): return lax.all_to_all(x, LL, split_axis=0, concat_axis=0, tiled=True)  22.2 us
    pallas_call x1, Pallas kernels, head(): pl.pallas_call(lambda *refs: head_kernel(*refs, half=half, levels=levels,...  7.35 us
    pallas_call x1, Pallas kernels, bases(): pl.pallas_call(lambda *refs: basis_kernel(*refs, cols=cols, blocks=blocks...  7.02 us
    ppermute x4, starting transfers between devices, swap(): return lax.ppermute(x, 'mem', SWAP)  6.6 us
    ppermute x4, waiting for transfers between devices, swap(): return lax.ppermute(x, 'mem', SWAP)  4.28 us
  transfers between devices with their start and end apart: 8, of which 3 were waited for; matrix products, arithmetic and copies ran while one was open for 1% of the time, Pallas kernels for 17%

profile of v1, /device:TPU:1, one launch (start us, length us, event | category | flops | bytes accessed | tf_op | source)
XLA Modules:
  0.0 156.5 jit_solution(1585698594858993715)
XLA Ops:
  0.0 7.4 %head.1 = bf16[64,240,128]{2,1,0:T(8,128)(2,1)} custom-call(bf16[3,4,90,16,128]{4,3,2,1,0:T(8,128)(2,1)} %bitcast.21, s32[64,128]{1,0:T(8,128)} %refs_1_.1, s32[64,128]{1,0:T(8,128)} %refs_2_.1, s32[64,128]{1,0:T(8,128)} %refs_3_.1, f32[64,128]{1,0:T(8,128)} %refs_4_.1), custom_call_target="tpu_custom_call" | custom-call | flops 6000000000 | bytes 1048576 | tf_op jit(solution)/shard_map/head/pallas_call | solution.py:190
  7.4 0.0 copy-start.3
  7.4 12.3 %all-to-all-start.1 = ((bf16[64,240,128]{2,1,0:T(8,128)(2,1)}), bf16[64,240,128]{2,1,0:T(8,128)(2,1)}, u32[]{:S(2)}, u32[]{:S(2)}) async-start(bf16[64,240,128]{2,1,0:T(8,128)(2,1)} %head.1), calls=%async_computation.1 | async-start | bytes 7864320 | tf_op jit(solution)/shard_map/all_to_all | solution.py:35
  19.7 0.0 copy-done.3
  19.8 2.4 %collective-permute-start.1 = (bf16[360,512]{1,0:T(8,128)(2,1)S(1)}, bf16[360,512]{1,0:T(8,128)(2,1)S(1)}, u32[]{:S(2)}, u32[]{:S(2)}) collective-permute-start(bf16[360,512]{1,0:T(8,128)(2,1)S(1)} %convert_bitcast_fusion.refs_1_), channel_id=1, source_target_pairs={{0,32},{1,97},{32,64},{33,1},{64,96},{65,33},{96,0},{97,65},{2,34}... | collective-permute-start | bytes 1105928 | tf_op jit(solution)/shard_map/ppermute | solution.py:619
  22.2 0.5 collective-permute-start.2
  22.7 0.6 pad_add_fusion.refs_0_
  23.3 3.0 %relayout_last.1 = bf16[64,96,128]{2,1,0:T(8,128)(2,1)} custom-call(s32[4]{0:T(128)} %pad_add_fusion.refs_0_, bf16[3,4,90,16,128]{4,3,2,1,0:T(8,128)(2,1)} %bitcast.22), custom_call_target="tpu_custom_call" | custom-call | tf_op jit(solution)/shard_map/relayout_last/pallas_call | solution.py:230
  26.3 44.1 %collective-permute-done.1 = bf16[360,512]{1,0:T(8,128)(2,1)S(1)} collective-permute-done((bf16[360,512]{1,0:T(8,128)(2,1)S(1)}, bf16[360,512]{1,0:T(8,128)(2,1)S(1)}, u32[]{:S(2)}, u32[]{:S(2)}) %collective-permute-start.1) | collective-permute-done | bytes 368672 | tf_op jit(solution)/shard_map/ppermute | solution.py:619
  70.4 0.0 collective-permute-done.2
  70.4 0.1 pad_maximum_fusion.refs_2_
  70.5 4.2 %collective-permute-start.3 = (bf16[3,360,256]{2,1,0:T(8,128)(2,1)S(1)}, bf16[3,360,256]{2,1,0:T(8,128)(2,1)S(1)}, u32[]{:S(2)}, u32[]{:S(2)}) collective-permute-start(bf16[3,360,256]{2,1,0:T(8,128)(2,1)S(1)} %pad_maximum_fusion.refs_2_), channel_id=1, source_target_pairs={{0,1},{1,0},{2,3},{3,2},{4,5},{5,4},{6,7},{7,6},{8,9},{9,8},{10,11... | collective-permute-start | bytes 1658888 | tf_op jit(solution)/shard_map/ppermute | solution.py:48
  74.7 0.0 all-to-all-done.1
  74.7 9.8 %all-to-all-start = ((bf16[64,96,128]{2,1,0:T(8,128)(2,1)}), bf16[64,96,128]{2,1,0:T(8,128)(2,1)}, u32[]{:S(2)}, u32[]{:S(2)}) async-start(bf16[64,96,128]{2,1,0:T(8,128)(2,1)} %relayout_last.1), calls=%async_computation | async-start | bytes 3145728 | tf_op jit(solution)/shard_map/all_to_all | solution.py:35
  84.6 1.2 slice.12
  85.8 0.0 copy-start.4
  85.8 0.0 copy-start
  85.8 0.6 collective-permute-start
  86.4 7.0 %bases.1 = (bf16[768,1536]{1,0:T(8,128)(2,1)}, bf16[1536,768]{1,0:T(8,128)(2,1)}, bf16[512,512]{1,0:T(8,128)(2,1)}, bf16[512,512]{1,0:T(8,128)(2,1)}) custom-call(), custom_call_target="tpu_custom_call" | custom-call | flops 12000000000 | bytes 1048576 | tf_op jit(solution)/shard_map/bases/pallas_call | solution.py:311
  93.4 0.0 copy-done.4
  93.4 0.0 collective-permute-done.3.refs_3_
  93.4 0.0 copy-done
  93.4 0.8 arrange.1.refs_4_
  94.3 0.0 copy-start.2
  94.3 1.1 copy-done.2
  95.4 0.0 collective-permute-done
  95.4 0.0 copy-start.5
  95.4 0.9 copy-done.5
  96.3 15.6 %member_pair.1.refs_9_ = bf16[4,16,96,128]{3,2,1,0:T(8,128)(2,1)} custom-call(s32[4]{0:T(128)} %pad_add_fusion.refs_0_, bf16[4,16,240,128]{3,2,1,0:T(8,128)(2,1)} %bitcast.14.refs_1_, bf16[4,16,48,128]{3,2,1,0:T(8,128)(2,1)} %bitcast.24, bf16[4,16,48,128]{3,2,1,0:T(8,128)(2,1)} %bitcast.27, bf16[4,1472,128]{2,1,0:T(8,128)(2,1)} %copy-done.2, ...), custom_call_target="tpu_custom_call" | custom-call | flops 12000000000 | bytes 1048576 | tf_op jit(solution)/shard_map/member_pair/pallas_call | solution.py:555
  112.0 0.0 all-to-all-done
  112.0 9.6 %member_last.1 = (bf16[4,16,48,128]{3,2,1,0:T(8,128)(2,1)}, bf16[4,16,48,128]{3,2,1,0:T(8,128)(2,1)}) custom-call(s32[4]{0:T(128)} %pad_add_fusion.refs_0_, bf16[4,16,96,128]{3,2,1,0:T(8,128)(2,1)} %bitcast.5.refs_1_, bf16[4,16,48,128]{3,2,1,0:T(8,128)(2,1)} %bitcast.25, bf16[4,16,48,128]{3,2,1,0:T(8,128)(2,1)} %bitcast.28, bf16[4,1472,128]{2,1,0:T(8,128)(2,1)} %copy-done.2, ...), custom_call_target="tpu_custom_call" | custom-call | flops 6000000000 | bytes 1048576 | tf_op jit(solution)/shard_map/member_last/pallas_call | solution.py:555
  121.6 0.2 collective-permute-start.4
  121.8 2.4 %collective-permute-done.4 = bf16[4,16,48,128]{3,2,1,0:T(8,128)(2,1)S(1)} collective-permute-done((bf16[4,16,48,128]{3,2,1,0:T(8,128)(2,1)}, bf16[4,16,48,128]{3,2,1,0:T(8,128)(2,1)S(1)}, u32[]{:S(2)}, u32[]{:S(2)}) %collective-permute-start.4) | collective-permute-done | bytes 786464 | tf_op jit(solution)/shard_map/ppermute | solution.py:48
  124.2 0.0 copy-start.1
  124.2 1.3 add_convert_fusion
  125.5 25.4 %all_to_all.15.refs_1_ = bf16[64,48,128]{2,1,0:T(8,128)(2,1)S(1)} all-to-all(bf16[64,48,128]{2,1,0:T(8,128)(2,1)S(1)} %bitcast.23), channel_id=1, replica_groups=mesh['lat'=4,'lon'=16,'mem'=2] {'lat','lon'}, dimensions={0} | all-to-all | bytes 1572864 | tf_op jit(solution)/shard_map/all_to_all | solution.py:35
  150.9 1.6 %collective-permute-start.5 = (bf16[64,48,128]{2,1,0:T(8,128)(2,1)S(1)}, bf16[64,48,128]{2,1,0:T(8,128)(2,1)S(1)}, u32[]{:S(2)}, u32[]{:S(2)}) collective-permute-start(bf16[64,48,128]{2,1,0:T(8,128)(2,1)S(1)} %all_to_all.15.refs_1_), channel_id=1, source_target_pairs={{0,1},{1,0},{2,3},{3,2},{4,5},{5,4},{6,7},{7,6},{8,9},{9,8},{10,11... | collective-permute-start | bytes 2359304 | tf_op jit(solution)/shard_map/ppermute | solution.py:48
  152.5 1.9 %collective-permute-done.5.refs_2_ = bf16[64,48,128]{2,1,0:T(8,128)(2,1)S(1)} collective-permute-done((bf16[64,48,128]{2,1,0:T(8,128)(2,1)S(1)}, bf16[64,48,128]{2,1,0:T(8,128)(2,1)S(1)}, u32[]{:S(2)}, u32[]{:S(2)}) %collective-permute-start.5) | collective-permute-done | bytes 786464 | tf_op jit(solution)/shard_map/ppermute | solution.py:48
  154.4 0.0 copy-done.1
  154.4 2.1 %finish.1 = f32[90,16,128]{2,1,0:T(8,128)} custom-call(s32[4]{0:T(128)S(1)} %copy-done.1, bf16[64,48,128]{2,1,0:T(8,128)(2,1)S(1)} %all_to_all.15.refs_1_, bf16[64,48,128]{2,1,0:T(8,128)(2,1)S(1)} %collective-permute-done.5.refs_2_), custom_call_target="tpu_custom_call" | custom-call | tf_op jit(solution)/shard_map/finish/pallas_call | solution.py:590
  (3 shorter events, 0.1 us)
Async XLA Ops:
  7.4 12.4 %copy-start.3 = (f32[1,360,512]{2,1,0:T(8,128)S(1)}, f32[1,360,512]{2,1,0:T(8,128)}, u32[]{:S(2)}) copy-start(f32[1,360,512]{2,1,0:T(8,128)} %param.7) | copy-start | bytes 2211844
  7.4 67.3 %all-to-all-start.1 = ((bf16[64,240,128]{2,1,0:T(8,128)(2,1)}), bf16[64,240,128]{2,1,0:T(8,128)(2,1)}, u32[]{:S(2)}, u32[]{:S(2)}) async-start(bf16[64,240,128]{2,1,0:T(8,128)(2,1)} %head.1), calls=%async_computation.1 | async-start | bytes 7864320 | tf_op jit(solution)/shard_map/all_to_all | solution.py:35
  19.8 50.6 %collective-permute-start.1 = (bf16[360,512]{1,0:T(8,128)(2,1)S(1)}, bf16[360,512]{1,0:T(8,128)(2,1)S(1)}, u32[]{:S(2)}, u32[]{:S(2)}) collective-permute-start(bf16[360,512]{1,0:T(8,128)(2,1)S(1)} %convert_bitcast_fusion.refs_1_), channel_id=1, source_target_pairs={{0,32},{1,97},{32,64},{33,1},{64,96},{65,33},{96,0},{97,65},{2,34}... | collective-permute-start | bytes 1105928 | tf_op jit(solution)/shard_map/ppermute | solution.py:619
  22.2 48.2 %collective-permute-start.2 = (bf16[360,256]{1,0:T(8,128)(2,1)S(1)}, bf16[360,256]{1,0:T(8,128)(2,1)S(1)}, u32[]{:S(2)}, u32[]{:S(2)}) collective-permute-start(bf16[360,256]{1,0:T(8,128)(2,1)S(1)} %fusion), channel_id=1, source_target_pairs={{0,64},{32,96},{64,0},{96,32},{1,65},{33,97},{65,1},{97,33},{2,66}... | collective-permute-start | bytes 552968 | tf_op jit(solution)/shard_map/ppermute | solution.py:39
  70.5 22.9 %collective-permute-start.3 = (bf16[3,360,256]{2,1,0:T(8,128)(2,1)S(1)}, bf16[3,360,256]{2,1,0:T(8,128)(2,1)S(1)}, u32[]{:S(2)}, u32[]{:S(2)}) collective-permute-start(bf16[3,360,256]{2,1,0:T(8,128)(2,1)S(1)} %pad_maximum_fusion.refs_2_), channel_id=1, source_target_pairs={{0,1},{1,0},{2,3},{3,2},{4,5},{5,4},{6,7},{7,6},{8,9},{9,8},{10,11... | collective-permute-start | bytes 1658888 | tf_op jit(solution)/shard_map/ppermute | solution.py:48
  74.7 37.3 %all-to-all-start = ((bf16[64,96,128]{2,1,0:T(8,128)(2,1)}), bf16[64,96,128]{2,1,0:T(8,128)(2,1)}, u32[]{:S(2)}, u32[]{:S(2)}) async-start(bf16[64,96,128]{2,1,0:T(8,128)(2,1)} %relayout_last.1), calls=%async_computation | async-start | bytes 3145728 | tf_op jit(solution)/shard_map/all_to_all | solution.py:35
  85.8 7.7 %copy-start.4 = (bf16[64,48,128]{2,1,0:T(8,128)(2,1)}, bf16[64,48,128]{2,1,0:T(8,128)(2,1)S(1)}, u32[]{:S(2)}) copy-start(bf16[64,48,128]{2,1,0:T(8,128)(2,1)S(1)} %slice.12) | copy-start | bytes 2359300
  85.8 7.7 %copy-start = (s32[4]{0:T(128)S(1)}, s32[4]{0:T(128)}, u32[]{:S(2)}) copy-start(s32[4]{0:T(128)} %pad_add_fusion.refs_0_) | copy-start | bytes 52
  85.8 9.6 %collective-permute-start = (bf16[64,48,128]{2,1,0:T(8,128)(2,1)S(1)}, bf16[64,48,128]{2,1,0:T(8,128)(2,1)S(1)}, u32[]{:S(2)}, u32[]{:S(2)}) collective-permute-start(bf16[64,48,128]{2,1,0:T(8,128)(2,1)S(1)} %slice.12), channel_id=1, source_target_pairs={{0,1},{1,0},{2,3},{3,2},{4,5},{5,4},{6,7},{7,6},{8,9},{9,8},{10,11... | collective-permute-start | bytes 2359304 | tf_op jit(solution)/shard_map/ppermute | solution.py:48
  94.3 1.1 copy-start.2
  95.4 0.9 copy-start.5
  121.6 2.6 %collective-permute-start.4 = (bf16[4,16,48,128]{3,2,1,0:T(8,128)(2,1)}, bf16[4,16,48,128]{3,2,1,0:T(8,128)(2,1)S(1)}, u32[]{:S(2)}, u32[]{:S(2)}) collective-permute-start(bf16[4,16,48,128]{3,2,1,0:T(8,128)(2,1)} %get-tuple-element.20), channel_id=1, source_target_pairs={{0,1},{1,0},{2,3},{3,2},{4,5},{5,4},{6,7},{7,6},{8,9},{9,8},{10,11... | collective-permute-start | bytes 2359304 | tf_op jit(solution)/shard_map/ppermute | solution.py:48
  124.2 30.2 %copy-start.1 = (s32[4]{0:T(128)S(1)}, s32[4]{0:T(128)}, u32[]{:S(2)}) copy-start(s32[4]{0:T(128)} %pad_add_fusion.refs_0_) | copy-start | bytes 52
  150.9 3.5 %collective-permute-start.5 = (bf16[64,48,128]{2,1,0:T(8,128)(2,1)S(1)}, bf16[64,48,128]{2,1,0:T(8,128)(2,1)S(1)}, u32[]{:S(2)}, u32[]{:S(2)}) collective-permute-start(bf16[64,48,128]{2,1,0:T(8,128)(2,1)S(1)} %all_to_all.15.refs_1_), channel_id=1, source_target_pairs={{0,1},{1,0},{2,3},{3,2},{4,5},{5,4},{6,7},{7,6},{8,9},{9,8},{10,11... | collective-permute-start | bytes 2359304 | tf_op jit(solution)/shard_map/ppermute | solution.py:48
